TPU v7x, 256 devices: a whole 4x4x8 slice. The times are simulated.
256 devices in a mesh: track: 4 (over y), ifg: 4 (over z_lo), pix: 16 (over z_hi, x, core).
Axes of the slice: x: 4, y: 4, z: 8 (z_hi: 2, z_lo: 4; z = z_hi * 4 + z_lo), core: 2. Of those that a mesh axis runs over, the one named last changes fastest.
Arguments:
- phases: bfloat16 [4, 600, 262144], P('track', 'ifg', 'pix')
- pairs: int32 [4, 600, 2], P('track', 'ifg'), may hold values from 0 to 249, as said below
- date_map: int32 [4, 250], replicated, may hold values from 0 to 319, as said below
- knots: int32 [32], replicated, may hold values from 0 to 319, as said below
- look: float32 [4, 3, 262144], P(None, None, 'pix'), may hold values from -1 to 1
Outputs:
- enu: float32 [3, 320, 262144], P(None, None, ('pix', 'ifg', 'track'))
- spline: float32 [3, 32, 262144], P(None, None, ('pix', 'ifg', 'track'))
Inputs may be any that keep to these rules, and one draw needn't show every extreme that they name: pairs[t, k, 0] < pairs[t, k, 1] <= pairs[t, k, 0] + 5. `date_map`: the dates of one track map to distinct epochs. `knots`: strictly increasing, the first 0 and the last 319.
All inputs are finite; a program needn't handle non-finite values.
Results may differ from a plain program's by a relative error of at most 0.0003.
Values may be sent and summed in bfloat16 or wider, within the bound.
A program may use at most 128 MiB of HBM per device.

v0:
```python
import jax
import jax.numpy as jnp
from jax import lax
from jax.sharding import PartitionSpec as P

EPOCHS = 320
damping = 0.5
ridge = 0.1
HIGH = lax.Precision.HIGHEST


def joined_along(tiles, dim):
    tiles = jnp.moveaxis(tiles, 0, dim)
    lengths = tiles.shape
    return tiles.reshape(*lengths[:dim], lengths[dim] * lengths[dim + 1], *lengths[dim + 2 :])


def from_everyone(value, axis):
    copies = jnp.broadcast_to(value, (lax.axis_size(axis), *value.shape))
    return lax.all_to_all(copies, axis, split_axis=0, concat_axis=0, tiled=True)


def collect(value, axis, dim):
    return joined_along(from_everyone(value, axis), dim)


def taken_together(value, axis):
    everything = from_everyone(value, axis)
    return jnp.sum(everything, axis=0)


def incidence(pair_rows, ndate):
    dates = jnp.arange(ndate, dtype=jnp.int32)[:, None]
    later = (dates == pair_rows[None, :, 1]).astype(jnp.float32)
    earlier = (dates == pair_rows[None, :, 0]).astype(jnp.float32)
    return later - earlier


def inverse_normal(normal_part):
    ndate = normal_part.shape[0]
    normal = normal_part + damping * jnp.eye(ndate, dtype=jnp.float32)
    factor = jnp.linalg.cholesky(normal)
    return jax.scipy.linalg.cho_solve((factor, True), jnp.eye(ndate, dtype=jnp.float32))


def hat_basis(knots, n_epochs):
    spots = knots.astype(jnp.float32)
    left = jnp.concatenate([spots[:1] - 1.0, spots[:-1]])
    right = jnp.concatenate([spots[1:], spots[-1:] + 1.0])
    epochs = jnp.arange(n_epochs, dtype=jnp.float32)[:, None]
    rise = (epochs - left) / (spots - left)
    fall = (right - epochs) / (right - spots)
    return jnp.maximum(0.0, jnp.minimum(rise, fall))


def geometry(series, date_map, look, knots, n_epochs):
    epochs = jnp.arange(n_epochs, dtype=jnp.int32)
    onehot = (date_map[:, None, :] == epochs[None, :, None]).astype(jnp.float32)
    seen = jnp.sum(onehot, axis=2)
    resampled = jnp.einsum("tcd,tdp->tcp", onehot, series, precision=HIGH)

    def entry(first, second):
        value = jnp.einsum("tc,tp->cp", seen, look[:, first] * look[:, second], precision=HIGH)
        if first == second:
            value = value + ridge
        return value

    a00, a01, a02 = (entry(0, 0), entry(0, 1), entry(0, 2))
    a11, a12, a22 = (entry(1, 1), entry(1, 2), entry(2, 2))
    b_all = [jnp.sum(look[:, i][:, None, :] * resampled, axis=0) for i in range(3)]
    c00 = a11 * a22 - a12 * a12
    c01 = a02 * a12 - a01 * a22
    c02 = a01 * a12 - a02 * a11
    c11 = a00 * a22 - a02 * a02
    c12 = a01 * a02 - a00 * a12
    c22 = a00 * a11 - a01 * a01
    det = a00 * c00 + a01 * c01 + a02 * c02
    east = (c00 * b_all[0] + c01 * b_all[1] + c02 * b_all[2]) / det
    north = (c01 * b_all[0] + c11 * b_all[1] + c12 * b_all[2]) / det
    upward = (c02 * b_all[0] + c12 * b_all[1] + c22 * b_all[2]) / det
    enu = jnp.stack([east, north, upward])
    basis = hat_basis(knots, n_epochs)
    gram = jnp.dot(basis.T, basis, precision=HIGH)
    factor = jnp.linalg.cholesky(gram)
    fitter = jax.scipy.linalg.cho_solve((factor, True), basis.T)
    spline = jnp.einsum("kc,icp->ikp", fitter, enu, precision=HIGH)
    return (enu, spline)


def shards(phases, pairs, date_map, knots, look):
    ndate = date_map.shape[1]
    n_epochs = hat_count()
    n_track = lax.axis_size("track")
    n_ifg = lax.axis_size("ifg")
    width = phases.shape[2] // (n_track * n_ifg)
    offset = lax.axis_index("ifg") * (width * n_track) + lax.axis_index("track") * width
    look_local = lax.dynamic_slice_in_dim(look, offset, width, 2)
    phase_rows = phases[0]
    pair_rows = pairs[0]
    phase_all = lax.all_to_all(phase_rows, "ifg", split_axis=1, concat_axis=0, tiled=True)
    pair_all = collect(pair_rows, "ifg", 0)
    incid = incidence(pair_all, ndate)
    normal_part = jnp.dot(incid, incid.T, precision=HIGH)
    rhs = jnp.dot(incid.astype(jnp.bfloat16), phase_all, preferred_element_type=jnp.float32)
    ninv = inverse_normal(normal_part)
    pixel_count = rhs.shape[1] * lax.axis_size("ifg") * lax.axis_size("pix")
    series = jnp.dot(ninv, rhs, precision=HIGH)
    total = taken_together(jnp.sum(series, axis=1), ("ifg", "pix"))
    series = series - (total / pixel_count)[:, None]
    gathered = lax.all_to_all(series[None], "track", split_axis=2, concat_axis=0, tiled=True)
    return geometry(gathered, date_map, look_local, knots, n_epochs)


def hat_count():
    return EPOCHS


def solution(mesh):
    in_specs = (P("track", "ifg", "pix"), P("track", "ifg", None), P(), P(), P(None, None, "pix"))
    out_specs = (P(None, None, ("pix", "ifg", "track")), P(None, None, ("pix", "ifg", "track")))
    return jax.shard_map(shards, mesh=mesh, in_specs=in_specs, out_specs=out_specs, check_vma=False)
```

profile of v0, /device:TPU:1, one launch (start us, length us, event | category | flops | bytes accessed | tf_op | source)
XLA Modules:
  0.0 270.9 jit_solution(16111083648875466656)
XLA Ops:
  0.6 1.3 broadcast_in_dim.9
  1.9 6.4 %all-to-all-start = ((s32[4,150,2]{1,2,0:T(2,128)}), s32[4,150,2]{1,2,0:T(2,128)S(1)}, u32[]{:S(2)}, u32[]{:S(2)}) async-start(s32[4,150,2]{1,2,0:T(2,128)} %broadcast_in_dim.9), calls=%async_computation | async-start | bytes 16384 | tf_op jit(solution)/shard_map/all_to_all | solution.py:20
  8.3 11.1 %all_to_all.35 = bf16[150,4,4096]{2,1,0:T(4,128)(2,1)} reshape(bf16[1,150,16384]{2,1,0:T(8,128)(2,1)} %param.5) | data formatting | bytes 9830400 | tf_op jit(solution)/shard_map/all_to_all | solution.py:100
  19.4 7.3 %copy.30 = bf16[150,4,4096]{2,0,1:T(8,128)(2,1)} copy(bf16[150,4,4096]{2,1,0:T(4,128)(2,1)} %all_to_all.35) | data formatting | bytes 9830400 | tf_op jit(solution)/shard_map/all_to_all | solution.py:100
  26.8 0.0 all-to-all-done
  26.8 5.4 %all-to-all-start.1 = ((bf16[150,4,4096]{2,0,1:T(8,128)(2,1)}), bf16[150,4,4096]{2,0,1:T(8,128)(2,1)}, u32[]{:S(2)}, u32[]{:S(2)}) async-start(bf16[150,4,4096]{2,0,1:T(8,128)(2,1)} %copy.30), calls=%async_computation.1 | async-start | bytes 9961472 | tf_op jit(solution)/shard_map/all_to_all | solution.py:100
  32.3 0.1 reshape.69
  32.4 1.0 fusion.3
  33.5 0.1 copy.29
  33.6 0.1 fusion.16
  33.7 11.7 %cholesky.63 = f32[128,128]{1,0:T(8,128)S(1)} custom-call(f32[128,128]{1,0:T(8,128)S(1)} %cholesky.156), custom_call_target="Cholesky" | custom-call | tf_op jit(solution)/shard_map/jit(cholesky)/cholesky | solution.py:42
  45.4 9.8 %custom-call.28 = f32[1,128,128]{1,2,0:T(8,128)S(1)} custom-call(f32[1,128,128]{2,1,0:T(8,128)S(1)} %get-tuple-element.40), custom_call_target="InvertDiagBlocksLowerTriangular" | custom-call | tf_op jit(solution)/shard_map/jit(cholesky)/cholesky | solution.py:42
  55.3 0.2 constant_dynamic-update-slice_fusion
  55.5 0.3 convolution_subtract_fusion.2
  55.7 11.2 %cholesky.133 = f32[122,122]{1,0:T(8,128)S(1)} custom-call(f32[122,122]{1,0:T(8,128)S(1)} %convolution_subtract_fusion.2), custom_call_target="Cholesky" | custom-call | tf_op jit(solution)/shard_map/jit(cholesky)/cholesky | solution.py:42
  66.9 0.6 compare_reduce_fusion.1
  67.6 0.6 compare_reduce_fusion.2
  69.6 0.1 fusion.21
  69.7 20.2 %custom-call.29 = f32[2,128,128]{1,2,0:T(8,128)S(1)} custom-call(f32[2,128,128]{2,1,0:T(8,128)S(1)} %pad_maximum_fusion.1), custom_call_target="InvertDiagBlocksLowerTriangular" | custom-call | tf_op jit(solution)/shard_map/jit(_cho_solve)/triangular_solve | solution.py:43
  89.9 0.3 fusion.17
  90.2 0.3 convolution_subtract_fusion.1
  90.4 0.3 fusion.27
  90.7 0.3 fusion.26
  91.0 0.3 convolution_subtract_fusion
  91.3 0.3 fusion.25
  91.6 50.3 %all-to-all-done.1 = bf16[150,4,4096]{2,0,1:T(8,128)(2,1)} async-done(((bf16[150,4,4096]{2,0,1:T(8,128)(2,1)}), bf16[150,4,4096]{2,0,1:T(8,128)(2,1)}, u32[]{:S(2)}, u32[]{:S(2)}) %all-to-all-start.1) | async-done | bytes 4915232 | tf_op jit(solution)/shard_map/all_to_all | solution.py:100
  141.9 6.0 %all_to_all.38 = bf16[600,4096]{1,0:T(8,128)(2,1)} reshape(bf16[4,150,4096]{2,1,0:T(8,128)(2,1)} %bitcast.11) | data formatting | bytes 9830400 | tf_op jit(solution)/shard_map/all_to_all | solution.py:100
  147.8 4.2 %fusion.5 = f32[250,4096]{1,0:T(8,128)S(1)} fusion(bf16[600,4096]{1,0:T(8,128)(2,1)} %all_to_all.38, s32[600]{0:T(1024)S(1)} %get-tuple-element.26, s32[600]{0:T(1024)S(1)} %get-tuple-element.25), kind=kOutput, calls=%fused_computation.31 | convolution fusion | flops 1229699968 | bytes 9016000 | tf_op jit(solution)/shard_map/dot_general | solution.py:104
  152.0 5.3 %fusion.48 = (f32[250]{0:T(256)S(1)}, f32[250,4096]{1,0:T(8,128)}) fusion(f32[250,4096]{1,0:T(8,128)S(1)} %fusion.5, f32[122,250]{1,0:T(8,128)S(1)} %fusion.26, f32[128,250]{1,0:T(8,128)S(1)} %fusion.25), kind=kOutput, calls=%fused_computation.113 | convolution fusion | flops 3073086208 | bytes 8443000 | tf_op jit(solution)/shard_map/dot_general | solution.py:107
  157.3 0.7 broadcast_in_dim.10
  158.0 10.5 %all-to-all-start.2 = ((f32[64,1,250]{2,1,0:T(1,128)}), f32[64,1,250]{2,1,0:T(1,128)S(1)}, u32[]{:S(2)}, u32[]{:S(2)}) async-start(f32[64,1,250]{2,1,0:T(1,128)} %broadcast_in_dim.10), calls=%async_computation.2 | async-start | bytes 131072 | tf_op jit(solution)/shard_map/all_to_all | solution.py:20
  168.5 0.1 fusion.47
  168.6 9.6 %all-to-all-done.2 = f32[64,1,250]{2,1,0:T(1,128)S(1)} async-done(((f32[64,1,250]{2,1,0:T(1,128)}), f32[64,1,250]{2,1,0:T(1,128)S(1)}, u32[]{:S(2)}, u32[]{:S(2)}) %all-to-all-start.2) | async-done | bytes 64032 | tf_op jit(solution)/shard_map/all_to_all | solution.py:20
  178.2 0.1 reduce_sum.56
  178.3 4.7 %subtract_bitcast_fusion = f32[1,250,4096]{2,1,0:T(8,128)} fusion(f32[250,4096]{1,0:T(8,128)} %get-tuple-element.50, f32[250]{0:T(256)S(1)} %broadcast_multiply_fusion), kind=kLoop, calls=%fused_computation.5 | loop fusion | flops 1024000 | bytes 8193000 | tf_op jit(solution)/shard_map/broadcast_in_dim | solution.py:110
  183.0 10.2 %copy.32 = f32[1,250,4096]{1,0,2:T(1,128)} copy(f32[1,250,4096]{2,1,0:T(8,128)} %subtract_bitcast_fusion) | data formatting | bytes 8192000 | tf_op jit(solution)/shard_map/broadcast_in_dim | solution.py:110
  193.2 5.0 %all-to-all-start.3 = ((f32[1,250,4096]{1,0,2:T(1,128)}), f32[1,250,4096]{1,0,2:T(1,128)}, u32[]{:S(2)}, u32[]{:S(2)}) async-start(f32[1,250,4096]{1,0,2:T(1,128)} %copy.32), calls=%async_computation.3 | async-start | bytes 8388608 | tf_op jit(solution)/shard_map/all_to_all | solution.py:110
  198.2 0.6 fusion.46
  200.1 0.1 convert_subtract_fusion.3
  200.2 0.4 fusion.20
  200.7 0.1 copy.34
  200.7 2.9 %cholesky.147 = f32[32,32]{1,0:T(8,128)S(1)} custom-call(f32[32,32]{1,0:T(8,128)S(1)} %fusion.33), custom_call_target="Cholesky" | custom-call | tf_op jit(solution)/shard_map/jit(cholesky)/cholesky | solution.py:84
  203.7 0.6 compare_reduce_fusion
  204.3 0.7 fusion.30
  205.0 2.4 custom-call.30
  207.4 0.8 dynamic-slice_bitcast_fusion.2
  208.2 0.3 fusion.19
  208.6 0.2 convolution_bitcast_fusion.1
  208.8 0.0 copy-done.4
  208.8 0.3 convert_reduce_fusion
  209.1 2.4 convolution_add_fusion
  211.4 2.4 convolution_add_fusion.1
  213.8 2.3 convolution_add_fusion.2
  216.1 1.2 fusion.35
  217.4 1.3 fusion.37
  218.7 28.1 %all-to-all-done.3 = f32[1,250,4096]{1,0,2:T(1,128)} async-done(((f32[1,250,4096]{1,0,2:T(1,128)}), f32[1,250,4096]{1,0,2:T(1,128)}, u32[]{:S(2)}, u32[]{:S(2)}) %all-to-all-start.3) | async-done | bytes 4096032 | tf_op jit(solution)/shard_map/all_to_all | solution.py:110
  246.8 4.4 %copy.35 = f32[1,250,4096]{1,2,0:T(8,128)} copy(f32[1,250,4096]{1,0,2:T(1,128)} %all-to-all-done.3) | data formatting | bytes 8192000
  251.2 5.6 %copy.33 = f32[1,250,4,1024]{3,1,2,0:T(8,128)} copy(f32[1,250,4,1024]{1,3,2,0:T(8,128)} %bitcast.84) | data formatting | bytes 8192000 | tf_op jit(solution)/shard_map/all_to_all | solution.py:110
  256.8 0.0 copy-start.3
  256.9 6.9 %multiply_reduce_fusion.2 = (f32[320,1024]{1,0:T(8,128)S(1)}, f32[320,1024]{1,0:T(8,128)S(1)}, f32[320,1024]{1,0:T(8,128)S(1)}) fusion(f32[4,1024]{1,0:T(4,128)S(1)} %get-tuple-element.36, f32[4,1024]{1,0:T(4,128)S(1)} %get-tuple-element.35, f32[4,1024]{1,0:T(4,128)S(1)} %get-tuple-element.34, f32[1,250,4,1024]{3,1,2,0:T(8,128)} %copy.33, ...), kind=kOutput, calls=%fused_computation.2 | convolution fusion | flops 3939361280 | bytes 8081312 | tf_op jit(solution)/shard_map/tcd,tdp->tcp/dot_general | solution.py:60
  263.8 3.0 %divide_bitcast_fusion.2 = (f32[1,320,1024]{2,1,0:T(8,128)S(1)}, f32[1,320,1024]{2,1,0:T(8,128)S(1)}, f32[1,320,1024]{2,1,0:T(8,128)S(1)}) fusion(f32[320,1024]{1,0:T(8,128)S(1)} %get-tuple-element.23, f32[320,1024]{1,0:T(8,128)S(1)} %get-tuple-element.24, f32[320,1024]{1,0:T(8,128)S(1)} %get-tuple-element.22, f32[320,1024]{1,0:T(8,128)S(1)} %copy-done.3, ...), kind=kOutput, calls=%fused_computation.13 | convolution fusion | flops 29167616 | bytes 14455808 | tf_op jit(solution)/shard_map/tc,tp->cp/dot_general | solution.py:63
  266.8 0.5 pad_maximum_fusion
  267.3 0.0 copy-start
  267.3 3.3 %convolution_bitcast_fusion = f32[3,32,1024]{2,1,0:T(8,128)} fusion(f32[3,320,1024]{2,1,0:T(8,128)S(1)} %pad_maximum_fusion, f32[32,320,1]{1,0,2:T(8,128)S(1)} %convolution_bitcast_fusion.1), kind=kOutput, calls=%fused_computation.20 | convolution fusion | flops 377487360 | bytes 4366336 | tf_op jit(solution)/shard_map/kc,icp->ikp/dot_general | solution.py:86
  (25 shorter events, 0.3 us)
Async XLA Ops:
  1.9 24.9 %all-to-all-start = ((s32[4,150,2]{1,2,0:T(2,128)}), s32[4,150,2]{1,2,0:T(2,128)S(1)}, u32[]{:S(2)}, u32[]{:S(2)}) async-start(s32[4,150,2]{1,2,0:T(2,128)} %broadcast_in_dim.9), calls=%async_computation | async-start | bytes 16384 | tf_op jit(solution)/shard_map/all_to_all | solution.py:20
  26.8 5.4 %copy-start.5 = (s32[32]{0:T(128)S(1)}, s32[32]{0:T(128)}, u32[]{:S(2)}) copy-start(s32[32]{0:T(128)} %param.8) | copy-start | bytes 388
  26.8 115.1 %all-to-all-start.1 = ((bf16[150,4,4096]{2,0,1:T(8,128)(2,1)}), bf16[150,4,4096]{2,0,1:T(8,128)(2,1)}, u32[]{:S(2)}, u32[]{:S(2)}) async-start(bf16[150,4,4096]{2,0,1:T(8,128)(2,1)} %copy.30), calls=%async_computation.1 | async-start | bytes 9961472 | tf_op jit(solution)/shard_map/all_to_all | solution.py:100
  158.0 20.2 %all-to-all-start.2 = ((f32[64,1,250]{2,1,0:T(1,128)}), f32[64,1,250]{2,1,0:T(1,128)S(1)}, u32[]{:S(2)}, u32[]{:S(2)}) async-start(f32[64,1,250]{2,1,0:T(1,128)} %broadcast_in_dim.10), calls=%async_computation.2 | async-start | bytes 131072 | tf_op jit(solution)/shard_map/all_to_all | solution.py:20
  193.2 53.6 %all-to-all-start.3 = ((f32[1,250,4096]{1,0,2:T(1,128)}), f32[1,250,4096]{1,0,2:T(1,128)}, u32[]{:S(2)}, u32[]{:S(2)}) async-start(f32[1,250,4096]{1,0,2:T(1,128)} %copy.32), calls=%async_computation.3 | async-start | bytes 8388608 | tf_op jit(solution)/shard_map/all_to_all | solution.py:110
  200.2 8.6 %copy-start.4 = (s32[4,250]{1,0:T(4,128)S(1)}, s32[4,250]{1,0:T(4,128)}, u32[]{:S(2)}) copy-start(s32[4,250]{1,0:T(4,128)} %param.7) | copy-start | bytes 12004
  256.8 6.9 %copy-start.1 = (f32[320,1024]{1,0:T(8,128)S(1)}, f32[320,1024]{1,0:T(8,128)}, u32[]{:S(2)}) copy-start(f32[320,1024]{1,0:T(8,128)} %convolution_add_fusion) | copy-start | bytes 3932164
  256.8 6.9 %copy-start.2 = (f32[320,1024]{1,0:T(8,128)S(1)}, f32[320,1024]{1,0:T(8,128)}, u32[]{:S(2)}) copy-start(f32[320,1024]{1,0:T(8,128)} %convolution_add_fusion.1) | copy-start | bytes 3932164
  256.8 6.9 %copy-start.3 = (f32[320,1024]{1,0:T(8,128)S(1)}, f32[320,1024]{1,0:T(8,128)}, u32[]{:S(2)}) copy-start(f32[320,1024]{1,0:T(8,128)} %convolution_add_fusion.2) | copy-start | bytes 3932164
  267.3 3.3 %copy-start = (f32[3,320,1024]{2,1,0:T(8,128)}, f32[3,320,1024]{2,1,0:T(8,128)S(1)}, u32[]{:S(2)}) copy-start(f32[3,320,1024]{2,1,0:T(8,128)S(1)} %pad_maximum_fusion) | copy-start | bytes 11796484
where the time goes:
time: 276 us; the launch traced here: 271 us
  waiting for transfers between devices  88 us (32%)
  other arithmetic  66.9 us (24%)
  local copies, waits for them, and re-layouts  48.4 us (18%)
  matrix products  36.4 us (13%)
  starting transfers between devices  27.3 us (10%)
  between operations  3.84 us (1%)
    all_to_all x1, waiting for transfers between devices, shards(): lax.all_to_all(phase_rows, 'ifg', split_axis=1, concat_axis=0, tiled=True)  50.3 us
    another operation x7, other arithmetic, inverse_normal(): factor = jnp.linalg.cholesky(normal)  34 us
    all_to_all x1, waiting for transfers between devices, shards(): lax.all_to_all(series[None], 'track', split_axis=2, concat_axis=0, tiled=...  28.1 us
    all_to_all x3, local copies, waits for them, and re-layouts, shards(): lax.all_to_all(phase_rows, 'ifg', split_axis=1, concat_axis=0, tiled=True)  24.4 us
    another operation x6, other arithmetic, inverse_normal(): jax.scipy.linalg.cho_solve((factor, True), jnp.eye(ndate, dtype=jnp.float...  20.3 us
    all_to_all x2, starting transfers between devices, from_everyone(): return lax.all_to_all(copies, axis, split_axis=0, concat_axis=0, tiled=True)  16.9 us
    dot_general x6, matrix products, entry(): jnp.einsum('tc,tp->cp', seen, look[:, first] * look[:, second], precision...  12.6 us
    broadcast_in_dim x1, local copies, waits for them, and re-layouts, shards(): series[None]  10.2 us
  transfers between devices with their start and end apart: 4, of which 3 were waited for; matrix products, arithmetic and copies ran while one was open for 31% of the time, Pallas kernels for 0%

commit v1 on v0

--- a/solution.py
+++ b/solution.py
@@ -7,6 +7,13 @@
 damping = 0.5
 ridge = 0.1
 HIGH = lax.Precision.HIGHEST
+
+
+def exchange_blocks(value, axis, split, join):
+    size = lax.axis_size(axis)
+    parts = jnp.stack(jnp.split(value, size, axis=split), axis=0)
+    parts = lax.all_to_all(parts, axis, split_axis=0, concat_axis=0)
+    return jnp.concatenate(parts, axis=join)
 
 
 def joined_along(tiles, dim):
@@ -107,7 +114,7 @@
     series = jnp.dot(ninv, rhs, precision=HIGH)
     total = taken_together(jnp.sum(series, axis=1), ("ifg", "pix"))
     series = series - (total / pixel_count)[:, None]
-    gathered = lax.all_to_all(series[None], "track", split_axis=2, concat_axis=0, tiled=True)
+    gathered = exchange_blocks(series[None], "track", 2, 0)
     return geometry(gathered, date_map, look_local, knots, n_epochs)
 
 

time: 276 us -> 260 us (0.942)
  local copies, waits for them, and re-layouts: 48.4 us -> 34.8 us
    broadcast_in_dim x1 -> x0, local copies, waits for them, and re-layouts: 10.2 us -> none  [shards(): series[None]]
    another operation x0 -> x2, local copies, waits for them, and re-layouts: none -> 6.7 us  [exchange_blocks(): parts = jnp.stack(jnp.split(value, size, axis=split), axis=0)]
    all_to_all x1 -> x0, local copies, waits for them, and re-layouts: 5.6 us -> none  [shards(): lax.all_to_all(series[None], 'track', split_axis=2, concat_axis=0, tiled=...]
    unnamed x13 -> x12, local copies, waits for them, and re-layouts: 4.46 us -> 0.02 us
  transfers between devices with their start and end apart: 4 -> 4, of which waited for: 3 -> 3; matrix products, arithmetic and copies ran while one was open for 31% -> 33% of each run, Pallas kernels for 0% -> 0%
where the time goes in v1:
time: 260 us; the launch traced here: 255 us
  waiting for transfers between devices  87.2 us (34%)
  other arithmetic  64.8 us (25%)
  matrix products  36.8 us (14%)
  local copies, waits for them, and re-layouts  34.8 us (13%)
  starting transfers between devices  27.6 us (11%)
  between operations  4.04 us (2%)
    all_to_all x1, waiting for transfers between devices, shards(): lax.all_to_all(phase_rows, 'ifg', split_axis=1, concat_axis=0, tiled=True)  50.6 us
    another operation x7, other arithmetic, inverse_normal(): factor = jnp.linalg.cholesky(normal)  34 us
    all_to_all x1, waiting for transfers between devices, exchange_blocks(): parts = lax.all_to_all(parts, axis, split_axis=0, concat_axis=0)  26.9 us
    all_to_all x3, local copies, waits for them, and re-layouts, shards(): lax.all_to_all(phase_rows, 'ifg', split_axis=1, concat_axis=0, tiled=True)  24.4 us
    another operation x6, other arithmetic, inverse_normal(): jax.scipy.linalg.cho_solve((factor, True), jnp.eye(ndate, dtype=jnp.float...  20 us
    all_to_all x2, starting transfers between devices, from_everyone(): return lax.all_to_all(copies, axis, split_axis=0, concat_axis=0, tiled=True)  16.9 us
    dot_general x6, matrix products, entry(): jnp.einsum('tc,tp->cp', seen, look[:, first] * look[:, second], precision...  12.8 us
    all_to_all x2, waiting for transfers between devices, from_everyone(): return lax.all_to_all(copies, axis, split_axis=0, concat_axis=0, tiled=True)  9.64 us
  transfers between devices with their start and end apart: 4, of which 3 were waited for; matrix products, arithmetic and copies ran while one was open for 33% of the time, Pallas kernels for 0%

profile of v1, /device:TPU:1, one launch (start us, length us, event | category | flops | bytes accessed | tf_op | source)
XLA Modules:
  0.0 255.3 jit_solution(13472195605626599987)
XLA Ops:
  0.6 1.3 broadcast_in_dim.9
  1.9 6.4 %all-to-all-start = ((s32[4,150,2]{1,2,0:T(2,128)}), s32[4,150,2]{1,2,0:T(2,128)S(1)}, u32[]{:S(2)}, u32[]{:S(2)}) async-start(s32[4,150,2]{1,2,0:T(2,128)} %broadcast_in_dim.9), calls=%async_computation | async-start | bytes 16384 | tf_op jit(solution)/shard_map/all_to_all | solution.py:27
  8.3 11.1 %all_to_all.25 = bf16[150,4,4096]{2,1,0:T(4,128)(2,1)} reshape(bf16[1,150,16384]{2,1,0:T(8,128)(2,1)} %param.5) | data formatting | bytes 9830400 | tf_op jit(solution)/shard_map/all_to_all | solution.py:107
  19.4 7.3 %copy.30 = bf16[150,4,4096]{2,0,1:T(8,128)(2,1)} copy(bf16[150,4,4096]{2,1,0:T(4,128)(2,1)} %all_to_all.25) | data formatting | bytes 9830400 | tf_op jit(solution)/shard_map/all_to_all | solution.py:107
  26.8 0.0 all-to-all-done
  26.8 5.6 %all-to-all-start.1 = ((bf16[150,4,4096]{2,0,1:T(8,128)(2,1)}), bf16[150,4,4096]{2,0,1:T(8,128)(2,1)}, u32[]{:S(2)}, u32[]{:S(2)}) async-start(bf16[150,4,4096]{2,0,1:T(8,128)(2,1)} %copy.30), calls=%async_computation.1 | async-start | bytes 9961472 | tf_op jit(solution)/shard_map/all_to_all | solution.py:107
  32.4 0.0 copy-done.5
  32.5 0.1 reshape.72
  32.7 1.0 fusion.4
  33.7 0.1 copy.29
  33.8 0.1 fusion.17
  33.9 11.7 %cholesky.63 = f32[128,128]{1,0:T(8,128)S(1)} custom-call(f32[128,128]{1,0:T(8,128)S(1)} %cholesky.156), custom_call_target="Cholesky" | custom-call | tf_op jit(solution)/shard_map/jit(cholesky)/cholesky | solution.py:49
  45.6 9.8 %custom-call.28 = f32[1,128,128]{1,2,0:T(8,128)S(1)} custom-call(f32[1,128,128]{2,1,0:T(8,128)S(1)} %get-tuple-element.44), custom_call_target="InvertDiagBlocksLowerTriangular" | custom-call | tf_op jit(solution)/shard_map/jit(cholesky)/cholesky | solution.py:49
  55.5 0.2 constant_dynamic-update-slice_fusion
  55.7 0.3 convolution_subtract_fusion.2
  56.0 11.2 %cholesky.133 = f32[122,122]{1,0:T(8,128)S(1)} custom-call(f32[122,122]{1,0:T(8,128)S(1)} %convolution_subtract_fusion.2), custom_call_target="Cholesky" | custom-call | tf_op jit(solution)/shard_map/jit(cholesky)/cholesky | solution.py:49
  67.2 0.6 compare_reduce_fusion.1
  67.8 0.6 compare_reduce_fusion.2
  69.8 0.1 fusion.22
  69.9 19.8 %custom-call.29 = f32[2,128,128]{1,2,0:T(8,128)S(1)} custom-call(f32[2,128,128]{2,1,0:T(8,128)S(1)} %pad_maximum_fusion.2), custom_call_target="InvertDiagBlocksLowerTriangular" | custom-call | tf_op jit(solution)/shard_map/jit(_cho_solve)/triangular_solve | solution.py:50
  89.8 0.3 fusion.18
  90.0 0.3 convolution_subtract_fusion.1
  90.3 0.3 fusion.28
  90.6 0.3 fusion.27
  90.9 0.3 convolution_subtract_fusion
  91.2 0.3 fusion.26
  91.5 50.6 %all-to-all-done.1 = bf16[150,4,4096]{2,0,1:T(8,128)(2,1)} async-done(((bf16[150,4,4096]{2,0,1:T(8,128)(2,1)}), bf16[150,4,4096]{2,0,1:T(8,128)(2,1)}, u32[]{:S(2)}, u32[]{:S(2)}) %all-to-all-start.1) | async-done | bytes 4915232 | tf_op jit(solution)/shard_map/all_to_all | solution.py:107
  142.1 6.0 %all_to_all.28 = bf16[600,4096]{1,0:T(8,128)(2,1)} reshape(bf16[4,150,4096]{2,1,0:T(8,128)(2,1)} %bitcast.11) | data formatting | bytes 9830400 | tf_op jit(solution)/shard_map/all_to_all | solution.py:107
  148.0 4.2 %fusion.6 = f32[250,4096]{1,0:T(8,128)S(1)} fusion(bf16[600,4096]{1,0:T(8,128)(2,1)} %all_to_all.28, s32[600]{0:T(1024)S(1)} %get-tuple-element.26, s32[600]{0:T(1024)S(1)} %get-tuple-element.25), kind=kOutput, calls=%fused_computation.37 | convolution fusion | flops 1229699968 | bytes 9016000 | tf_op jit(solution)/shard_map/dot_general | solution.py:111
  152.3 5.3 %fusion.49 = (f32[250]{0:T(256)S(1)}, f32[250,4096]{1,0:T(8,128)}) fusion(f32[250,4096]{1,0:T(8,128)S(1)} %fusion.6, f32[122,250]{1,0:T(8,128)S(1)} %fusion.27, f32[128,250]{1,0:T(8,128)S(1)} %fusion.26), kind=kOutput, calls=%fused_computation.119 | convolution fusion | flops 3073086208 | bytes 8443000 | tf_op jit(solution)/shard_map/dot_general | solution.py:114
  157.5 0.7 broadcast_in_dim.10
  158.2 10.5 %all-to-all-start.2 = ((f32[64,1,250]{2,1,0:T(1,128)}), f32[64,1,250]{2,1,0:T(1,128)S(1)}, u32[]{:S(2)}, u32[]{:S(2)}) async-start(f32[64,1,250]{2,1,0:T(1,128)} %broadcast_in_dim.10), calls=%async_computation.2 | async-start | bytes 131072 | tf_op jit(solution)/shard_map/all_to_all | solution.py:27
  168.7 0.1 fusion.48
  168.7 9.6 %all-to-all-done.2 = f32[64,1,250]{2,1,0:T(1,128)S(1)} async-done(((f32[64,1,250]{2,1,0:T(1,128)}), f32[64,1,250]{2,1,0:T(1,128)S(1)}, u32[]{:S(2)}, u32[]{:S(2)}) %all-to-all-start.2) | async-done | bytes 64032 | tf_op jit(solution)/shard_map/all_to_all | solution.py:27
  178.4 0.1 reduce_sum.56
  178.5 2.6 %subtract_bitcast_fusion = f32[1,250,4096]{2,1,0:T(8,128)S(1)} fusion(f32[250,4096]{1,0:T(8,128)} %get-tuple-element.54, f32[250]{0:T(256)S(1)} %broadcast_multiply_fusion), kind=kLoop, calls=%fused_computation.7 | loop fusion | flops 1024000 | bytes 8193000 | tf_op jit(solution)/shard_map/broadcast_in_dim | solution.py:117
  181.1 0.6 slice_bitcast_fusion.3
  181.7 0.3 pad_maximum_fusion
  182.0 6.1 %copy.32 = f32[4,1,250,1024]{3,1,2,0:T(1,128)} copy(f32[4,1,250,1024]{3,2,1,0:T(8,128)S(1)} %pad_maximum_fusion) | data formatting | bytes 8192000 | tf_op jit(solution)/shard_map/stack | solution.py:14
  188.2 5.0 %all-to-all-start.3 = ((f32[4,1,250,1024]{3,1,2,0:T(1,128)}), f32[4,1,250,1024]{3,1,2,0:T(1,128)}, u32[]{:S(2)}, u32[]{:S(2)}) async-start(f32[4,1,250,1024]{3,1,2,0:T(1,128)} %copy.32), calls=%async_computation.3 | async-start | bytes 8192000 | tf_op jit(solution)/shard_map/all_to_all | solution.py:15
  193.2 0.6 fusion.47
  195.1 0.1 convert_subtract_fusion.3
  195.2 0.4 fusion.21
  195.6 0.1 copy.33
  195.7 2.9 %cholesky.147 = f32[32,32]{1,0:T(8,128)S(1)} custom-call(f32[32,32]{1,0:T(8,128)S(1)} %fusion.34), custom_call_target="Cholesky" | custom-call | tf_op jit(solution)/shard_map/jit(cholesky)/cholesky | solution.py:91
  198.7 0.6 compare_reduce_fusion
  199.3 0.7 fusion.31
  200.0 2.4 custom-call.30
  202.4 0.8 dynamic-slice_bitcast_fusion.2
  203.2 0.3 fusion.20
  203.5 0.2 convolution_bitcast_fusion.1
  203.7 0.0 copy-done.4
  203.7 0.3 convert_reduce_fusion
  204.0 2.3 convolution_add_fusion
  206.3 2.4 convolution_add_fusion.1
  208.8 2.3 convolution_add_fusion.2
  211.1 1.2 fusion.36
  212.3 1.3 fusion.38
  213.6 26.9 %all-to-all-done.3 = f32[4,1,250,1024]{3,1,2,0:T(1,128)} async-done(((f32[4,1,250,1024]{3,1,2,0:T(1,128)}), f32[4,1,250,1024]{3,1,2,0:T(1,128)}, u32[]{:S(2)}, u32[]{:S(2)}) %all-to-all-start.3) | async-done | bytes 4096032 | tf_op jit(solution)/shard_map/all_to_all | solution.py:15
  240.5 7.1 %multiply_reduce_fusion.2 = (f32[320,1024]{1,0:T(8,128)S(1)}, f32[320,1024]{1,0:T(8,128)S(1)}, f32[320,1024]{1,0:T(8,128)S(1)}) fusion(f32[4,1024]{1,0:T(4,128)S(1)} %get-tuple-element.40, f32[4,1024]{1,0:T(4,128)S(1)} %get-tuple-element.39, f32[4,1024]{1,0:T(4,128)S(1)} %get-tuple-element.38, f32[4,1,250,1024]{3,1,2,0:T(1,128)} %all-to-all-done.3, ...), kind=kOutput, calls=%fused_computation.2 | convolution fusion | flops 3939361280 | bytes 8081312 | tf_op jit(solution)/shard_map/tcd,tdp->tcp/dot_general | solution.py:67
  247.7 3.3 %divide_bitcast_fusion.2 = (f32[1,320,1024]{2,1,0:T(8,128)S(1)}, f32[1,320,1024]{2,1,0:T(8,128)S(1)}, f32[1,320,1024]{2,1,0:T(8,128)S(1)}) fusion(f32[320,1024]{1,0:T(8,128)S(1)} %get-tuple-element.23, f32[320,1024]{1,0:T(8,128)S(1)} %get-tuple-element.24, f32[320,1024]{1,0:T(8,128)S(1)} %get-tuple-element.22, f32[320,1024]{1,0:T(8,128)S(1)} %copy-done.3, ...), kind=kOutput, calls=%fused_computation.15 | convolution fusion | flops 29167616 | bytes 14455808 | tf_op jit(solution)/shard_map/tc,tp->cp/dot_general | solution.py:70
  250.9 0.5 pad_maximum_fusion.1
  251.5 0.0 copy-start
  251.5 3.3 %convolution_bitcast_fusion = f32[3,32,1024]{2,1,0:T(8,128)} fusion(f32[3,320,1024]{2,1,0:T(8,128)S(1)} %pad_maximum_fusion.1, f32[32,320,1]{1,0,2:T(8,128)S(1)} %convolution_bitcast_fusion.1), kind=kOutput, calls=%fused_computation.22 | convolution fusion | flops 377487360 | bytes 4366336 | tf_op jit(solution)/shard_map/kc,icp->ikp/dot_general | solution.py:93
  (25 shorter events, 0.3 us)
Async XLA Ops:
  1.9 24.9 %all-to-all-start = ((s32[4,150,2]{1,2,0:T(2,128)}), s32[4,150,2]{1,2,0:T(2,128)S(1)}, u32[]{:S(2)}, u32[]{:S(2)}) async-start(s32[4,150,2]{1,2,0:T(2,128)} %broadcast_in_dim.9), calls=%async_computation | async-start | bytes 16384 | tf_op jit(solution)/shard_map/all_to_all | solution.py:27
  26.8 5.7 %copy-start.5 = (s32[32]{0:T(128)S(1)}, s32[32]{0:T(128)}, u32[]{:S(2)}) copy-start(s32[32]{0:T(128)} %param.8) | copy-start | bytes 388
  26.8 115.3 %all-to-all-start.1 = ((bf16[150,4,4096]{2,0,1:T(8,128)(2,1)}), bf16[150,4,4096]{2,0,1:T(8,128)(2,1)}, u32[]{:S(2)}, u32[]{:S(2)}) async-start(bf16[150,4,4096]{2,0,1:T(8,128)(2,1)} %copy.30), calls=%async_computation.1 | async-start | bytes 9961472 | tf_op jit(solution)/shard_map/all_to_all | solution.py:107
  158.2 20.2 %all-to-all-start.2 = ((f32[64,1,250]{2,1,0:T(1,128)}), f32[64,1,250]{2,1,0:T(1,128)S(1)}, u32[]{:S(2)}, u32[]{:S(2)}) async-start(f32[64,1,250]{2,1,0:T(1,128)} %broadcast_in_dim.10), calls=%async_computation.2 | async-start | bytes 131072 | tf_op jit(solution)/shard_map/all_to_all | solution.py:27
  188.2 52.3 %all-to-all-start.3 = ((f32[4,1,250,1024]{3,1,2,0:T(1,128)}), f32[4,1,250,1024]{3,1,2,0:T(1,128)}, u32[]{:S(2)}, u32[]{:S(2)}) async-start(f32[4,1,250,1024]{3,1,2,0:T(1,128)} %copy.32), calls=%async_computation.3 | async-start | bytes 8192000 | tf_op jit(solution)/shard_map/all_to_all | solution.py:15
  195.2 8.6 %copy-start.4 = (s32[4,250]{1,0:T(4,128)S(1)}, s32[4,250]{1,0:T(4,128)}, u32[]{:S(2)}) copy-start(s32[4,250]{1,0:T(4,128)} %param.7) | copy-start | bytes 12004
  240.5 7.1 %copy-start.1 = (f32[320,1024]{1,0:T(8,128)S(1)}, f32[320,1024]{1,0:T(8,128)}, u32[]{:S(2)}) copy-start(f32[320,1024]{1,0:T(8,128)} %convolution_add_fusion) | copy-start | bytes 3932164
  240.5 7.1 %copy-start.2 = (f32[320,1024]{1,0:T(8,128)S(1)}, f32[320,1024]{1,0:T(8,128)}, u32[]{:S(2)}) copy-start(f32[320,1024]{1,0:T(8,128)} %convolution_add_fusion.1) | copy-start | bytes 3932164
  240.5 7.2 %copy-start.3 = (f32[320,1024]{1,0:T(8,128)S(1)}, f32[320,1024]{1,0:T(8,128)}, u32[]{:S(2)}) copy-start(f32[320,1024]{1,0:T(8,128)} %convolution_add_fusion.2) | copy-start | bytes 3932164
  251.5 3.3 %copy-start = (f32[3,320,1024]{2,1,0:T(8,128)}, f32[3,320,1024]{2,1,0:T(8,128)S(1)}, u32[]{:S(2)}) copy-start(f32[3,320,1024]{2,1,0:T(8,128)S(1)} %pad_maximum_fusion.1) | copy-start | bytes 11796484
